TPU v7x, 32 devices: a whole 2x2x4 slice. The times are simulated.
32 devices in a mesh: leaf: 8 (over z, x), vec: 4 (over y, core).
Axes of the slice: x: 2, y: 2, z: 4, core: 2. Of those that a mesh axis runs over, the one named last changes fastest.
Arguments:
- samples: bfloat16 [64, 32768], P('vec', 'leaf'), may hold values from -6 to 6
- coords: float32 [3, 32768], P(None, 'leaf'), may hold values from -4 to 4
- panel_area: float32 [32768], P('leaf'), may hold values from 0.05 to 0.5
- quad_weight: float32 [32768], P('leaf'), may hold values from 0.2 to 1
- leaf_basis: bfloat16 [128, 64, 256], P('leaf'), may hold values from -0.375 to 0.375
- transfer: bfloat16 [64, 2, 64, 64], P('leaf'), may hold values from -0.5 to 0.5
- coupling_fine: bfloat16 [128, 16, 64, 64], P('leaf'), may hold values from -0.1875 to 0.1875
- coupling_coarse: bfloat16 [64, 16, 64, 64], P('leaf'), may hold values from -0.1875 to 0.1875
- near_list: int32 [128, 16], P('leaf'), may hold values from 0 to 127, as said below
- send_fine: int32 [64, 32], P('leaf'), may hold values from 0 to 15
- send_coarse: int32 [64, 16], P('leaf'), may hold values from 0 to 7
- far_fine: int32 [128, 16], P('leaf'), may hold values from 0 to 255, as said below
- far_coarse: int32 [64, 16], P('leaf'), may hold values from 0 to 127, as said below
Outputs:
- sample_out: bfloat16 [64, 32768], P('vec', 'leaf')
- sample_gram: float32 [128, 64, 64], P('leaf', 'vec')
Inputs may be any that keep to these rules, and one draw needn't show every extreme that they name: `near_list`: row g names 16 different leaves, each at most 16 leaves from g. `send_fine`: row e * 8 + d names clusters of device e, counted on e from 0; every slot carries one. `send_coarse`: row e * 8 + d names clusters of device e, counted on e from 0; every slot carries one. `far_fine`: the rows of one device's 16 leaves name each of the values 0 to 255 exactly once. `far_coarse`: the rows of one device's parents name each of the values 0 to 127 exactly once.
All inputs are finite; a program needn't handle non-finite values.
Results may differ from a plain program's by a relative error of at most 0.0085.
Values may be sent and summed in bfloat16 or wider, within the bound.
A program may use at most 64 MiB of HBM per device.

v0:
```python
import functools
import jax
import jax.numpy as jnp
from jax import lax
from jax.experimental import pallas as pl
from jax.experimental.pallas import tpu as pltpu
from jax.sharding import PartitionSpec as P

four_pi = 4.0 * 3.141592653589793
NT = (((1,), (1,)), ((), ()))
MESH = pl.DeviceIdType.MESH


def pieces(block):
    first = block.astype(jnp.bfloat16).astype(jnp.float32)
    rest = block - first
    second = rest.astype(jnp.bfloat16).astype(jnp.float32)
    return first, second, rest - second


def main_kernel(
    near_ref, farf_ref, farc_ref,
    coords_ref, area_ref, weight_ref, sam_ref, send_ref, transfer_ref, basis_ref, cf_hbm, cc_hbm,
    out_ref, gram_ref,
    geo_ref, near_all, geo_low, geo_high, sam_low, sam_high, fine_all, coarse_all, got, got_smem, cf_ref, cc_ref,
    yfeat, xfeat, wvec, rows_all,
    halo_send, halo_recv, table_send, table_recv, fine_send, fine_recv, coarse_send, coarse_recv,
    rows_send, rows_recv, local_sem,
    *, caps,
):
    cap0, cap1 = caps
    leaf_dev, basis_rank, leaf_pts = basis_ref.shape
    vec_dev = sam_ref.shape[0]
    parents = leaf_dev // 2
    nb = farf_ref.shape[1]
    nbc = farc_ref.shape[1]
    nn = near_ref.shape[1]
    devices, vecs = lax.axis_size("leaf"), lax.axis_size("vec")
    me, row = lax.axis_index("leaf"), lax.axis_index("vec")

    def leaf_peer(step):
        return {"leaf": lax.rem(me + step, devices)}

    def vec_peer(step):
        return {"vec": lax.rem(row + step, vecs)}

    def remote(src, dst, send, recv, peer):
        return pltpu.make_async_remote_copy(
            src_ref=src, dst_ref=dst, send_sem=send, recv_sem=recv,
            device_id=peer, device_id_type=MESH,
        )

    def cut(leaf):
        return pl.ds(pl.multiple_of(leaf * leaf_pts, leaf_pts), leaf_pts)

    def nt(a, b):
        return lax.dot_general(a, b, NT, preferred_element_type=jnp.float32)

    load_fine = pltpu.make_async_copy(cf_hbm, cf_ref, local_sem.at[0])
    load_coarse = pltpu.make_async_copy(cc_hbm, cc_ref, local_sem.at[1])
    load_fine.start()
    load_coarse.start()

    def geometry(leaf, carry):
        xyz = coords_ref[:, cut(leaf)]
        norm = jnp.sum(xyz * xyz, axis=0, keepdims=True) + area_ref[:, cut(leaf)]
        weight = weight_ref[:, cut(leaf)] * (1.0 / four_pi)
        geo_ref[:, cut(leaf)] = jnp.concatenate(
            [xyz, norm, jnp.ones_like(norm), weight, jnp.zeros_like(xyz[:2])], axis=0
        )
        return carry

    lax.fori_loop(0, leaf_dev, geometry, 0, unroll=4)
    barrier = pltpu.get_barrier_semaphore()

    def greet(step, carry):
        pl.semaphore_signal(barrier, inc=1, device_id=leaf_peer(step), device_id_type=MESH)
        return carry

    lax.fori_loop(1, devices, greet, 0)
    for step in range(1, vecs):
        pl.semaphore_signal(barrier, inc=1, device_id=vec_peer(step), device_id_type=MESH)
    pl.semaphore_wait(barrier, devices - 1 + vecs - 1)

    def halos(side, geo_dst, sam_dst):
        peer = leaf_peer(1 if side == 0 else devices - 1)
        return (
            remote(geo_ref, geo_dst, halo_send.at[side, 0], halo_recv.at[side, 0], peer),
            remote(sam_ref, sam_dst, halo_send.at[side, 1], halo_recv.at[side, 1], peer),
        )

    @pl.when(me < devices - 1)
    def _():
        for copy in halos(0, geo_low, sam_low):
            copy.start()

    @pl.when(me > 0)
    def _():
        for copy in halos(1, geo_high, sam_high):
            copy.start()

    def table_copy(step):
        peer = lax.rem(me + step, devices)
        return remote(
            send_ref.at[peer], got.at[me], table_send.at[step], table_recv.at[step], {"leaf": peer}
        )

    def fine_copy(step):
        part = fine_all.at[pl.ds(me * leaf_dev, leaf_dev)]
        return remote(part, part, fine_send.at[step], fine_recv.at[step], leaf_peer(step))

    def coarse_copy(step):
        part = coarse_all.at[pl.ds(me * parents, parents)]
        return remote(part, part, coarse_send.at[step], coarse_recv.at[step], leaf_peer(step))

    def start_table(step, carry):
        table_copy(step).start()
        return carry

    lax.fori_loop(1, devices, start_table, 0)
    got[me] = send_ref[me]

    def fine_row(leaf, carry):
        coef = nt(sam_ref[:, cut(leaf)], basis_ref[leaf])
        fine_all[me * leaf_dev + leaf] = coef.astype(jnp.bfloat16)
        return carry

    lax.fori_loop(0, leaf_dev, fine_row, 0, unroll=4)

    def coarse_row(m, carry):
        child = me * leaf_dev + 2 * m
        coef = jnp.dot(fine_all[child], transfer_ref[m, 0], preferred_element_type=jnp.float32)
        coef += jnp.dot(fine_all[child + 1], transfer_ref[m, 1], preferred_element_type=jnp.float32)
        coarse_all[me * parents + m] = coef.astype(jnp.bfloat16)
        return carry

    lax.fori_loop(0, parents, coarse_row, 0, unroll=2)

    def prepare(part, geo_src, sam_src):
        def source(leaf, carry):
            geo = geo_src[:, cut(leaf)]
            y1, y2, y3 = pieces(geo)
            rows = jnp.concatenate([y1, y1, y1, y2, y2, y3], axis=0)
            yfeat[part * leaf_dev + leaf] = rows.T.astype(jnp.bfloat16)
            scaled = sam_src[:, cut(leaf)].astype(jnp.float32) * geo[5:6]
            wvec[part * leaf_dev + leaf] = scaled.astype(jnp.bfloat16)
            return carry

        lax.fori_loop(0, leaf_dev, source, 0, unroll=4)

    prepare(1, geo_ref, sam_ref)

    def target(leaf, carry):
        xyz = geo_ref[0:3, cut(leaf)]
        norm = jnp.sum(xyz * xyz, axis=0, keepdims=True)
        x8 = jnp.concatenate(
            [-2.0 * xyz, jnp.ones_like(norm), norm, jnp.zeros_like(xyz)], axis=0
        )
        x1, x2, x3 = pieces(x8)
        xfeat[leaf] = jnp.concatenate([x1, x2, x3, x1, x2, x1], axis=0).astype(jnp.bfloat16)
        return carry

    lax.fori_loop(0, leaf_dev, target, 0, unroll=2)

    @pl.when(me > 0)
    def _():
        for copy in halos(0, geo_low, sam_low):
            copy.wait_recv()
        prepare(0, geo_low, sam_low)

    @pl.when(me < devices - 1)
    def _():
        for copy in halos(1, geo_high, sam_high):
            copy.wait_recv()
        prepare(2, geo_high, sam_high)

    def start_fine(step, carry):
        fine_copy(step).start()
        return carry

    lax.fori_loop(1, devices, start_fine, 0)

    def start_coarse(step, carry):
        coarse_copy(step).start()
        return carry

    lax.fori_loop(1, devices, start_coarse, 0)

    def near_sum(leaf):
        features = xfeat[leaf]

        def step(group, total):
            for lane in range(4):
                offset = near_ref[leaf, group * 4 + lane] - (me - 1) * leaf_dev
                chosen = jnp.clip(offset, 0, 3 * leaf_dev - 1)
                dist = jnp.dot(yfeat[chosen], features, preferred_element_type=jnp.float32)
                block = lax.rsqrt(dist.astype(jnp.bfloat16))
                total = total + jnp.dot(wvec[chosen], block, preferred_element_type=jnp.float32)
            return total

        zero = jnp.zeros((vec_dev, leaf_pts), jnp.float32)
        return lax.fori_loop(0, nn // 4, step, zero)

    def near_leaf(leaf, carry):
        near_all[leaf] = near_sum(leaf)
        return carry

    lax.fori_loop(0, leaf_dev, near_leaf, 0)

    def finish(step, carry):
        table_copy(step).wait()
        fine_copy(step).wait()
        coarse_copy(step).wait()
        return carry

    lax.fori_loop(1, devices, finish, 0)
    to_smem = pltpu.make_async_copy(got, got_smem, local_sem.at[2])
    to_smem.start()
    load_fine.wait()
    load_coarse.wait()
    to_smem.wait()

    def rows_copy(m, step):
        part = rows_all.at[row, :, pl.ds(pl.multiple_of(m * 2 * leaf_pts, 2 * leaf_pts), 2 * leaf_pts)]
        return remote(part, part, rows_send.at[step, m], rows_recv.at[step, m], vec_peer(step))

    def parent(m, carry):
        coarse = None
        for b in range(nbc):
            slot = farc_ref[m, b]
            source = lax.div(slot, cap1)
            index = source * parents + got_smem[source, 0, cap0 + lax.rem(slot, cap1)]
            term = nt(coarse_all[index], cc_ref[m, b])
            coarse = term if coarse is None else coarse + term
        coarse = coarse.astype(jnp.bfloat16)
        for s in range(2):
            leaf = 2 * m + s
            field = nt(coarse, transfer_ref[m, s])
            for b in range(nb):
                slot = farf_ref[leaf, b]
                source = lax.div(slot, cap0)
                index = source * leaf_dev + got_smem[source, 0, lax.rem(slot, cap0)]
                field = field + nt(fine_all[index], cf_ref[leaf, b])
            local = field.astype(jnp.bfloat16)
            far = jnp.dot(local, basis_ref[leaf], preferred_element_type=jnp.float32)
            result = (near_all[leaf] + far).astype(out_ref.dtype)
            rows_all[row, :, cut(leaf)] = result
            out_ref[:, cut(leaf)] = result
        for step in range(1, vecs):
            rows_copy(m, step).start()
        return carry

    lax.fori_loop(0, parents, parent, 0)

    @pl.when(me < devices - 1)
    def _():
        for copy in halos(0, geo_low, sam_low):
            copy.wait_send()

    @pl.when(me > 0)
    def _():
        for copy in halos(1, geo_high, sam_high):
            copy.wait_send()

    def gram_pair(m, carry):
        for step in range(1, vecs):
            rows_copy(m, step).wait()
        for s in range(2):
            leaf = 2 * m + s
            everyone = rows_all[:, :, cut(leaf)].reshape(vecs * vec_dev, leaf_pts)
            gram_ref[leaf] = nt(rows_all[row, :, cut(leaf)], everyone) * (1.0 / leaf_pts)
        return carry

    lax.fori_loop(0, parents, gram_pair, 0)


def per_device(
    samples, coords, panel_area, quad_weight, leaf_basis, transfer,
    coupling_fine, coupling_coarse, near_list, send_fine, send_coarse, far_fine, far_coarse,
):
    vec_dev, points = samples.shape
    leaf_dev, basis_rank, leaf_pts = leaf_basis.shape
    parents = leaf_dev // 2
    devices, vecs = lax.axis_size("leaf"), lax.axis_size("vec")
    caps = (send_fine.shape[1], send_coarse.shape[1])
    send = jnp.concatenate([send_fine, send_coarse], axis=1)
    width = -(-send.shape[1] // 128) * 128
    send = jnp.pad(send, ((0, 0), (0, width - send.shape[1]))).reshape(devices, 1, width)
    smem = pl.BlockSpec(memory_space=pltpu.SMEM)
    vmem = pl.BlockSpec(memory_space=pltpu.VMEM)
    hbm = pl.BlockSpec(memory_space=pl.ANY)
    bf16 = jnp.bfloat16
    dma = pltpu.SemaphoreType.DMA
    sample_out, gram = pl.pallas_call(
        functools.partial(main_kernel, caps=caps),
        out_shape=(
            jax.ShapeDtypeStruct((vec_dev, points), bf16),
            jax.ShapeDtypeStruct((leaf_dev, vec_dev, vecs * vec_dev), jnp.float32),
        ),
        in_specs=[smem] * 3 + [vmem] * 7 + [hbm] * 2,
        out_specs=(vmem, vmem),
        scratch_shapes=[
            pltpu.VMEM((8, points), jnp.float32),
            pltpu.VMEM((leaf_dev, vec_dev, leaf_pts), jnp.float32),
            pltpu.VMEM((8, points), jnp.float32),
            pltpu.VMEM((8, points), jnp.float32),
            pltpu.VMEM(samples.shape, bf16),
            pltpu.VMEM(samples.shape, bf16),
            pltpu.VMEM((devices * leaf_dev, vec_dev, basis_rank), bf16),
            pltpu.VMEM((devices * parents, vec_dev, basis_rank), bf16),
            pltpu.VMEM(send.shape, jnp.int32),
            pltpu.SMEM(send.shape, jnp.int32),
            pltpu.VMEM(coupling_fine.shape, bf16),
            pltpu.VMEM(coupling_coarse.shape, bf16),
            pltpu.VMEM((3 * leaf_dev, leaf_pts, 48), bf16),
            pltpu.VMEM((leaf_dev, 48, leaf_pts), bf16),
            pltpu.VMEM((3 * leaf_dev, vec_dev, leaf_pts), bf16),
            pltpu.VMEM((vecs, vec_dev, points), bf16),
            dma((2, 2)), dma((2, 2)),
            dma((devices,)), dma((devices,)),
            dma((devices,)), dma((devices,)),
            dma((devices,)), dma((devices,)),
            dma((vecs, parents)), dma((vecs, parents)),
            dma((3,)),
        ],
        compiler_params=pltpu.CompilerParams(
            vmem_limit_bytes=56 * 1024 * 1024, collective_id=0, has_side_effects=True
        ),
    )(
        near_list, far_fine, far_coarse,
        coords, panel_area[None, :], quad_weight[None, :], samples, send, transfer, leaf_basis, coupling_fine, coupling_coarse,
    )
    return sample_out, gram


def solution(mesh):
    return jax.shard_map(
        per_device,
        mesh=mesh,
        in_specs=(
            P("vec", "leaf"), P(None, "leaf"), P("leaf"), P("leaf"),
            P("leaf", None, None), P("leaf", None, None, None),
            P("leaf", None, None, None), P("leaf", None, None, None),
            P("leaf", None), P("leaf", None), P("leaf", None), P("leaf", None), P("leaf", None),
        ),
        out_specs=(P("vec", "leaf"), P("leaf", "vec", None)),
        check_vma=False,
    )
```

profile of v0, /device:TPU:3, one launch (start us, length us, event | category | flops | bytes accessed | tf_op | source)
XLA Modules:
  0.0 77.8 jit_solution(2971559526790253481)
XLA Ops:
  0.6 0.8 %pad_add_fusion = s32[8,48]{1,0:T(8,128)S(1)} fusion(s32[8,16]{1,0:T(8,128)} %param.23, s32[8,32]{1,0:T(8,128)} %param.22), kind=kLoop, calls=%fused_computation | loop fusion | flops 384 | bytes 3072 | tf_op jit(solution)/shard_map/concatenate | solution.py:286
  1.4 0.6 pad.4
  2.0 72.7 %shard_map.140 = (bf16[16,4096]{1,0:T(8,128)(2,1)}, f32[16,16,64]{2,1,0:T(8,128)}) custom-call(s32[16,16]{1,0:T(8,128)} %near_ref.1, s32[16,16]{1,0:T(8,128)} %farf_ref.1, s32[8,16]{1,0:T(8,128)} %farc_ref.1, f32[3,4096]{1,0:T(4,128)} %coords_ref.1, f32[1,4096]{1,0:T(1,128)} %bitcast.3, f32[1,4096]{1,0:T(1,128)} %bitcast.4, bf16[16,4096]{1,0:T(8,128)(2,1)} %sam_ref.1, ...), custom_call_target="tpu_custom_call" | custom-call | tf_op jit(solution)/shard_map/pallas_call | solution.py:294
  74.7 1.6 %copy.17 = bf16[16,4096]{1,0:T(8,128)(2,1)} copy(bf16[16,4096]{1,0:T(8,128)(2,1)} %get-tuple-element.4) | data formatting | bytes 262144
  76.2 1.6 %copy.18 = f32[16,16,64]{2,1,0:T(8,128)} copy(f32[16,16,64]{2,1,0:T(8,128)} %get-tuple-element.5) | data formatting | bytes 131072
where the time goes:
time: 78.3 us; the launch traced here: 77.8 us
  Pallas kernels  72.7 us (93%)
  local copies, waits for them, and re-layouts  3.73 us (5%)
    pallas_call x1, Pallas kernels, per_device(): pl.pallas_call(functools.partial(main_kernel, caps=caps), out_shape=(jax....  72.7 us
    unnamed x2, local copies, waits for them, and re-layouts  3.14 us

commit v1 on v0

v1 whole, which is shorter than its diff:
```python
import functools
import jax
import jax.numpy as jnp
from jax import lax
from jax.experimental import pallas as pl
from jax.experimental.pallas import tpu as pltpu
from jax.sharding import PartitionSpec as P

four_pi = 4.0 * 3.141592653589793
NT = (((1,), (1,)), ((), ()))
MESH = pl.DeviceIdType.MESH
LAG = 4


def pieces(block):
    first = block.astype(jnp.bfloat16).astype(jnp.float32)
    rest = block - first
    second = rest.astype(jnp.bfloat16).astype(jnp.float32)
    return first, second, rest - second


def main_kernel(
    near_ref, farf_ref, farc_ref,
    coords_ref, area_ref, weight_ref, sam_ref, sendf_ref, sendc_ref, transfer_ref, basis_ref, cf_hbm, cc_hbm,
    out_ref, gram_ref,
    geo_all, wvec, table, got, got_smem, coef_pk, fine_all, coarse_all, cf_ref, cc_ref,
    yfeat, xfeat, near_all, rows_all, gram_out,
    geo_send, geo_recv, geo_fsend, geo_frecv, sam_send, sam_recv, sam_fsend, sam_frecv,
    table_send, table_recv, coef_send, coef_recv, coef_fsend, coef_frecv,
    rows_send, rows_recv, out_send, out_recv, gram_send, gram_recv, local_sem,
):
    leaf_dev, basis_rank, leaf_pts = basis_ref.shape
    vec_dev = sam_ref.shape[0]
    parents = leaf_dev // 2
    cap0, cap1 = sendf_ref.shape[1], sendc_ref.shape[1]
    nb = farf_ref.shape[1]
    nbc = farc_ref.shape[1]
    nn = near_ref.shape[1]
    half_leaves, half_parents = leaf_dev // 2, parents // 2
    both = 2 * vec_dev
    devices, vecs = lax.axis_size("leaf"), lax.axis_size("vec")
    groups = vecs // 2
    me, row = lax.axis_index("leaf"), lax.axis_index("vec")
    h, g = lax.rem(row, 2), lax.div(row, 2)
    partner = {"vec": row + 1 - 2 * h}
    first_leaf, first_parent = h * half_leaves, h * half_parents

    def leaf_peer(step):
        return {"leaf": lax.rem(me + step, devices)}

    def group_peer(step):
        return {"vec": lax.rem(g + step, groups) * 2 + h}

    def remote(src, dst, send, recv, peer):
        return pltpu.make_async_remote_copy(
            src_ref=src, dst_ref=dst, send_sem=send, recv_sem=recv,
            device_id=peer, device_id_type=MESH,
        )

    def cut(leaf):
        return pl.ds(pl.multiple_of(leaf * leaf_pts, leaf_pts), leaf_pts)

    def nt(a, b):
        return lax.dot_general(a, b, NT, preferred_element_type=jnp.float32)

    barrier = pltpu.get_barrier_semaphore()

    def greet(step, carry):
        pl.semaphore_signal(barrier, inc=1, device_id=leaf_peer(step), device_id_type=MESH)
        return carry

    lax.fori_loop(1, devices, greet, 0)
    pl.semaphore_signal(barrier, inc=1, device_id=partner, device_id_type=MESH)
    for step in range(1, groups):
        pl.semaphore_signal(barrier, inc=1, device_id=group_peer(step), device_id_type=MESH)

    load_fine = pltpu.make_async_copy(cf_hbm.at[pl.ds(first_leaf, half_leaves)], cf_ref, local_sem.at[0])
    load_coarse = pltpu.make_async_copy(cc_hbm.at[pl.ds(first_parent, half_parents)], cc_ref, local_sem.at[1])
    load_fine.start()
    load_coarse.start()

    def own(leaf, carry):
        xyz = coords_ref[:, cut(leaf)]
        norm = jnp.sum(xyz * xyz, axis=0, keepdims=True) + area_ref[:, cut(leaf)]
        geo_all[leaf_dev + leaf] = jnp.concatenate([xyz, norm], axis=0)
        weight = weight_ref[:, cut(leaf)] * (1.0 / four_pi)
        scaled = sam_ref[:, cut(leaf)].astype(jnp.float32) * weight
        wvec[leaf_dev + leaf, h] = scaled.astype(jnp.bfloat16)
        return carry

    lax.fori_loop(0, leaf_dev, own, 0, unroll=4)
    table[...] = jnp.zeros_like(table)

    def fill(d, carry):
        table[d, 0:1, 0:cap0] = sendf_ref[pl.ds(d, 1), :]
        table[d, 1:2, 0:cap1] = sendc_ref[pl.ds(d, 1), :]
        return carry

    lax.fori_loop(0, devices, fill, 0)
    got[me] = table[me]
    pl.semaphore_wait(barrier, devices - 1 + 1 + groups - 1)

    def sides(run):
        @pl.when(me < devices - 1)
        def _():
            run(0, leaf_peer(1))

        @pl.when(me > 0)
        def _():
            run(1, leaf_peer(devices - 1))

    def geo_copy(side, peer):
        src = geo_all.at[pl.ds(leaf_dev + first_leaf, half_leaves)]
        dst = geo_all.at[pl.ds(side * 2 * leaf_dev + first_leaf, half_leaves)]
        return remote(src, dst, geo_send.at[side], geo_recv.at[side], peer)

    def geo_forward(side):
        part = geo_all.at[pl.ds(side * 2 * leaf_dev + first_leaf, half_leaves)]
        return remote(part, part, geo_fsend.at[side], geo_frecv.at[side], partner)

    def sam_copy(side, peer):
        src = wvec.at[pl.ds(leaf_dev, leaf_dev), h]
        dst = wvec.at[pl.ds(side * 2 * leaf_dev, leaf_dev), h]
        return remote(src, dst, sam_send.at[side], sam_recv.at[side], peer)

    def sam_forward(part):
        block = wvec.at[pl.ds(part * leaf_dev, leaf_dev), h]
        return remote(block, block, sam_fsend.at[part], sam_frecv.at[part], partner)

    def table_copy(step):
        peer = lax.rem(me + step, devices)
        return remote(table.at[peer], got.at[me], table_send.at[step], table_recv.at[step], {"leaf": peer})

    def coef_copy(step):
        part = coef_pk.at[me, :, h]
        return remote(part, part, coef_send.at[step], coef_recv.at[step], leaf_peer(step))

    def coef_forward(step):
        part = coef_pk.at[lax.rem(me - step + devices, devices), :, h]
        return remote(part, part, coef_fsend.at[step], coef_frecv.at[step], partner)

    sides(lambda side, peer: geo_copy(side, peer).start())
    sides(lambda side, peer: sam_copy(side, peer).start())
    sam_forward(1).start()

    def start_table(step, carry):
        table_copy(step).start()
        return carry

    lax.fori_loop(1, devices, start_table, 0)

    blank = jnp.zeros((basis_rank, leaf_pts), jnp.bfloat16)
    packed = []
    for m in range(parents):
        left = jnp.concatenate([basis_ref[2 * m], blank], axis=0)
        right = jnp.concatenate([blank, basis_ref[2 * m + 1]], axis=0)
        coef = nt(sam_ref[:, cut(2 * m)], left) + nt(sam_ref[:, cut(2 * m + 1)], right)
        coef = coef.astype(jnp.bfloat16)
        coef_pk[me, m, h] = coef
        packed.append(coef)
    coarse = []
    for m in range(parents):
        both_children = transfer_ref[m].reshape(2 * basis_rank, basis_rank)
        coarse.append(jnp.dot(packed[m], both_children, preferred_element_type=jnp.float32))
    for m in range(half_parents):
        pair = jnp.concatenate([coarse[2 * m], coarse[2 * m + 1]], axis=1)
        coef_pk[me, parents + m, h] = pair.astype(jnp.bfloat16)

    def prepare(part):
        def source(leaf, carry):
            geo = geo_all[part * leaf_dev + leaf]
            ones = jnp.ones((1, leaf_pts), jnp.float32)
            rows = jnp.concatenate([geo, ones, jnp.zeros((3, leaf_pts), jnp.float32)], axis=0)
            y1, y2, y3 = pieces(rows)
            rows = jnp.concatenate([y1, y1, y1, y2, y2, y3], axis=0)
            yfeat[part * leaf_dev + leaf] = rows.T.astype(jnp.bfloat16)
            return carry

        lax.fori_loop(0, leaf_dev, source, 0, unroll=4)

    prepare(1)

    def target(leaf, carry):
        xyz = geo_all[leaf_dev + first_leaf + leaf][0:3]
        norm = jnp.sum(xyz * xyz, axis=0, keepdims=True)
        x8 = jnp.concatenate(
            [-2.0 * xyz, jnp.ones_like(norm), norm, jnp.zeros_like(xyz)], axis=0
        )
        x1, x2, x3 = pieces(x8)
        features = jnp.concatenate([x1, x2, x3, x1, x2, x1], axis=0).astype(jnp.bfloat16)
        xfeat[0, leaf] = features
        xfeat[1, leaf] = features
        return carry

    lax.fori_loop(0, half_leaves, target, 0, unroll=2)

    def start_coef(step, carry):
        coef_copy(step).start()
        return carry

    def incoming(run):
        @pl.when(me > 0)
        def _():
            run(0)

        @pl.when(me < devices - 1)
        def _():
            run(1)

    def pass_geo(side):
        geo_copy(side, leaf_peer(0)).wait_recv()
        geo_forward(side).start()

    def use_geo(side):
        geo_forward(side).wait_recv()
        prepare(2 * side)

    def pass_sam(side):
        sam_copy(side, leaf_peer(0)).wait_recv()
        sam_forward(2 * side).start()

    incoming(pass_geo)
    incoming(use_geo)
    coef_forward(0).start()
    lax.fori_loop(1, devices, start_coef, 0)
    incoming(pass_sam)
    sam_forward(1).wait_recv()
    incoming(lambda side: sam_forward(2 * side).wait_recv())

    def near_leaf(leaf, carry):
        features = [xfeat[0, leaf], xfeat[1, leaf]]
        total = [None, None]
        base = (me - 1) * leaf_dev
        picked = [
            jnp.clip(near_ref[first_leaf + leaf, n] - base, 0, 3 * leaf_dev - 1) for n in range(nn)
        ]
        dists = {}
        for n in range(nn + LAG):
            if n < nn:
                dists[n] = jnp.dot(yfeat[picked[n]], features[n % 2], preferred_element_type=jnp.float32)
            m = n - LAG
            if m >= 0:
                block = lax.rsqrt(dists.pop(m).astype(jnp.bfloat16))
                values = wvec[picked[m]].reshape(both, leaf_pts)
                term = jnp.dot(values, block, preferred_element_type=jnp.float32)
                total[m % 2] = term if total[m % 2] is None else total[m % 2] + term
        near_all[0, leaf] = total[0]
        near_all[1, leaf] = total[1]
        return carry

    lax.fori_loop(0, half_leaves - 2, near_leaf, 0)

    def pass_coef(step, carry):
        coef_copy(step).wait_recv()
        coef_forward(step).start()
        return carry

    lax.fori_loop(1, devices, pass_coef, 0)
    lax.fori_loop(half_leaves - 2, half_leaves, near_leaf, 0)

    coef_forward(0).wait_recv()

    def finish(step, carry):
        table_copy(step).wait()
        coef_copy(step).wait_send()
        coef_forward(step).wait_recv()
        return carry

    lax.fori_loop(1, devices, finish, 0)
    to_smem = pltpu.make_async_copy(got, got_smem, local_sem.at[2])
    to_smem.start()

    def unpack(d, carry):
        for m in range(parents):
            pair = coef_pk[d, m].reshape(both, 2 * basis_rank)
            fine_all[d * leaf_dev + 2 * m] = pair[:, :basis_rank]
            fine_all[d * leaf_dev + 2 * m + 1] = pair[:, basis_rank:]
        for m in range(half_parents):
            pair = coef_pk[d, parents + m].reshape(both, 2 * basis_rank)
            coarse_all[d * parents + 2 * m] = pair[:, :basis_rank]
            coarse_all[d * parents + 2 * m + 1] = pair[:, basis_rank:]
        return carry

    lax.fori_loop(0, devices, unpack, 0)
    load_fine.wait()
    load_coarse.wait()
    to_smem.wait()

    def fine_term(leaf, b):
        slot = farf_ref[first_leaf + leaf, b]
        source = lax.div(slot, cap0)
        index = source * leaf_dev + got_smem[source, 0, lax.rem(slot, cap0)]
        return nt(fine_all[index], cf_ref[leaf, b])

    def coarse_term(m, b):
        slot = farc_ref[first_parent + m, b]
        source = lax.div(slot, cap1)
        index = source * parents + got_smem[source, 1, lax.rem(slot, cap1)]
        return nt(coarse_all[index], cc_ref[m, b])

    def rows_copy(m, step):
        part = rows_all.at[g, :, :, pl.ds(pl.multiple_of(m * 2 * leaf_pts, 2 * leaf_pts), 2 * leaf_pts)]
        return remote(part, part, rows_send.at[step, m], rows_recv.at[step, m], group_peer(step))

    def out_copy(m):
        columns = pl.ds(pl.multiple_of(m * 2 * leaf_pts, 2 * leaf_pts), 2 * leaf_pts)
        start = (first_leaf + 2 * m) * leaf_pts
        there = pl.ds(pl.multiple_of(start, 2 * leaf_pts), 2 * leaf_pts)
        return remote(
            rows_all.at[g, 1 - h, :, columns], out_ref.at[:, there], out_send.at[m], out_recv.at[m], partner
        )

    coarse_field = []
    for m in range(half_parents):
        field = coarse_term(m, 0)
        for b in range(1, nbc):
            field = field + coarse_term(m, b)
        coarse_field.append(field.astype(jnp.bfloat16))
    locals_ = []
    for leaf in range(half_leaves):
        field = nt(coarse_field[leaf // 2], transfer_ref[first_parent + leaf // 2, leaf % 2])
        for b in range(nb):
            field = field + fine_term(leaf, b)
        locals_.append(field.astype(jnp.bfloat16))
    for m in range(half_parents):
        for leaf in (2 * m, 2 * m + 1):
            far = jnp.dot(locals_[leaf], basis_ref[first_leaf + leaf], preferred_element_type=jnp.float32)
            result = (near_all[0, leaf] + near_all[1, leaf] + far).astype(out_ref.dtype)
            result = result.reshape(2, vec_dev, leaf_pts)
            rows_all[g, :, :, cut(leaf)] = result
        for step in range(1, groups):
            rows_copy(m, step).start()
        out_copy(m).start()

    for leaf in range(half_leaves):
        out_ref[:, cut(first_leaf + leaf)] = rows_all[g, h, :, cut(leaf)]

    def gram_pair(m, carry):
        for step in range(1, groups):
            rows_copy(m, step).wait()
        for s in range(2):
            leaf = 2 * m + s
            everyone = rows_all[:, :, :, cut(leaf)].reshape(vecs * vec_dev, leaf_pts)
            gram_ref[first_leaf + leaf] = nt(rows_all[g, h, :, cut(leaf)], everyone) * (1.0 / leaf_pts)
            gram_out[leaf] = nt(rows_all[g, 1 - h, :, cut(leaf)], everyone) * (1.0 / leaf_pts)
        return carry

    lax.fori_loop(0, half_parents, gram_pair, 0)
    gram_copy = remote(
        gram_out, gram_ref.at[pl.ds(first_leaf, half_leaves)], gram_send.at[0], gram_recv.at[0], partner
    )
    gram_copy.start()

    sides(lambda side, peer: geo_copy(side, peer).wait_send())
    sides(lambda side, peer: sam_copy(side, peer).wait_send())
    incoming(lambda side: geo_forward(side).wait_send())
    incoming(lambda side: sam_forward(2 * side).wait_send())
    sam_forward(1).wait_send()

    def drain(step, carry):
        coef_forward(step).wait_send()
        return carry

    lax.fori_loop(0, devices, drain, 0)
    for m in range(half_parents):
        out_copy(m).wait()
    gram_copy.wait()


def per_device(
    samples, coords, panel_area, quad_weight, leaf_basis, transfer,
    coupling_fine, coupling_coarse, near_list, send_fine, send_coarse, far_fine, far_coarse,
):
    vec_dev, points = samples.shape
    leaf_dev, basis_rank, leaf_pts = leaf_basis.shape
    parents, half = leaf_dev // 2, leaf_dev // 2
    devices, vecs = lax.axis_size("leaf"), lax.axis_size("vec")
    groups, both = vecs // 2, 2 * vec_dev
    nb, nbc = coupling_fine.shape[1], coupling_coarse.shape[1]
    smem = pl.BlockSpec(memory_space=pltpu.SMEM)
    vmem = pl.BlockSpec(memory_space=pltpu.VMEM)
    hbm = pl.BlockSpec(memory_space=pl.ANY)
    bf16, f32 = jnp.bfloat16, jnp.float32
    dma = pltpu.SemaphoreType.DMA
    sample_out, gram = pl.pallas_call(
        main_kernel,
        out_shape=(
            jax.ShapeDtypeStruct((vec_dev, points), bf16),
            jax.ShapeDtypeStruct((leaf_dev, vec_dev, vecs * vec_dev), f32),
        ),
        in_specs=[smem] * 3 + [vmem] * 8 + [hbm] * 2,
        out_specs=(vmem, vmem),
        scratch_shapes=[
            pltpu.VMEM((3 * leaf_dev, 4, leaf_pts), f32),
            pltpu.VMEM((3 * leaf_dev, 2, vec_dev, leaf_pts), bf16),
            pltpu.VMEM((devices, 2, 128), jnp.int32),
            pltpu.VMEM((devices, 2, 128), jnp.int32),
            pltpu.SMEM((devices, 2, 128), jnp.int32),
            pltpu.VMEM((devices, parents + parents // 2, 2, vec_dev, 2 * basis_rank), bf16),
            pltpu.VMEM((devices * leaf_dev, both, basis_rank), bf16),
            pltpu.VMEM((devices * parents, both, basis_rank), bf16),
            pltpu.VMEM((half, nb, basis_rank, basis_rank), bf16),
            pltpu.VMEM((half // 2, nbc, basis_rank, basis_rank), bf16),
            pltpu.VMEM((3 * leaf_dev, leaf_pts, 48), bf16),
            pltpu.VMEM((2, half, 48, leaf_pts), bf16),
            pltpu.VMEM((2, half, both, leaf_pts), f32),
            pltpu.VMEM((groups, 2, vec_dev, half * leaf_pts), bf16),
            pltpu.VMEM((half, vec_dev, vecs * vec_dev), f32),
            dma((2,)), dma((2,)), dma((2,)), dma((2,)),
            dma((2,)), dma((2,)), dma((3,)), dma((3,)),
            dma((devices,)), dma((devices,)),
            dma((devices,)), dma((devices,)), dma((devices,)), dma((devices,)),
            dma((groups, half // 2)), dma((groups, half // 2)),
            dma((half // 2,)), dma((half // 2,)),
            dma((1,)), dma((1,)),
            dma((3,)),
        ],
        compiler_params=pltpu.CompilerParams(
            vmem_limit_bytes=56 * 1024 * 1024, collective_id=0, has_side_effects=True
        ),
    )(
        near_list, far_fine, far_coarse,
        coords, panel_area[None, :], quad_weight[None, :], samples, send_fine, send_coarse,
        transfer, leaf_basis, coupling_fine, coupling_coarse,
    )
    return sample_out, gram


def solution(mesh):
    return jax.shard_map(
        per_device,
        mesh=mesh,
        in_specs=(
            P("vec", "leaf"), P(None, "leaf"), P("leaf"), P("leaf"),
            P("leaf", None, None), P("leaf", None, None, None),
            P("leaf", None, None, None), P("leaf", None, None, None),
            P("leaf", None), P("leaf", None), P("leaf", None), P("leaf", None), P("leaf", None),
        ),
        out_specs=(P("vec", "leaf"), P("leaf", "vec", None)),
        check_vma=False,
    )
```

time: 78.3 us -> 39.8 us (0.51)
  the two profiles are of different devices: /device:TPU:3 before, /device:TPU:11 now
where the time goes in v1:
time: 39.8 us; the launch traced here: 39.6 us
  Pallas kernels  35.9 us (90%)
  local copies, waits for them, and re-layouts  3.14 us (8%)
  between operations  0.64 us (2%)
    pallas_call x1, Pallas kernels, per_device(): pl.pallas_call(main_kernel, out_shape=(jax.ShapeDtypeStruct((vec_dev, poi...  35.9 us
    unnamed x2, local copies, waits for them, and re-layouts  3.14 us

profile of v1, /device:TPU:11, one launch (start us, length us, event | category | flops | bytes accessed | tf_op | source)
XLA Modules:
  0.0 39.6 jit_solution(8276097781409957193)
XLA Ops:
  0.6 35.9 %shard_map.140 = (bf16[16,4096]{1,0:T(8,128)(2,1)}, f32[16,16,64]{2,1,0:T(8,128)}) custom-call(s32[16,16]{1,0:T(8,128)} %near_ref.1, s32[16,16]{1,0:T(8,128)} %farf_ref.1, s32[8,16]{1,0:T(8,128)} %farc_ref.1, f32[3,4096]{1,0:T(4,128)} %coords_ref.1, f32[1,4096]{1,0:T(1,128)} %bitcast.2, f32[1,4096]{1,0:T(1,128)} %bitcast.3, bf16[16,4096]{1,0:T(8,128)(2,1)} %sam_ref.1, ...), custom_call_target="tpu_custom_call" | custom-call | tf_op jit(solution)/shard_map/pallas_call | solution.py:385
  36.5 1.6 %copy.17 = bf16[16,4096]{1,0:T(8,128)(2,1)} copy(bf16[16,4096]{1,0:T(8,128)(2,1)} %get-tuple-element.4) | data formatting | bytes 262144
  38.1 1.6 %copy.18 = f32[16,16,64]{2,1,0:T(8,128)} copy(f32[16,16,64]{2,1,0:T(8,128)} %get-tuple-element.5) | data formatting | bytes 131072

commit v2 on v1

v2 whole, which is shorter than its diff:
```python
import functools
import jax
import jax.numpy as jnp
from jax import lax
from jax.experimental import pallas as pl
from jax.experimental.pallas import tpu as pltpu
from jax.sharding import PartitionSpec as P

four_pi = 4.0 * 3.141592653589793
NT = (((1,), (1,)), ((), ()))
MESH = pl.DeviceIdType.MESH
LAG = 4
CHUNKS = 4
MATE_AT, FAR_AT = 1, 2


def pieces(block):
    first = block.astype(jnp.bfloat16).astype(jnp.float32)
    rest = block - first
    second = rest.astype(jnp.bfloat16).astype(jnp.float32)
    return first, second, rest - second


def main_kernel(
    near_hbm, farf_hbm, farc_hbm,
    coords_hbm, area_hbm, weight_hbm, sam_hbm, sendf_hbm, sendc_hbm, transfer_hbm, basis_hbm, cf_hbm, cc_hbm,
    out_ref, gram_ref,
    near_ref, farf_ref, farc_ref,
    coords_ref, area_ref, weight_ref, sam_ref, sendf_ref, sendc_ref, transfer_ref, basis_ref,
    geo_all, wvec, table, got, got_smem, coef_pk, fine_all, coarse_all, cf_ref, cc_ref,
    yfeat, xfeat, near_all, local_ref, rows_all, gram_out,
    geo_send, geo_recv, geo_fsend, geo_frecv, sam_send, sam_recv, sam_fsend, sam_frecv, own_send, own_recv,
    table_send, table_recv, coef_send, coef_recv, mate_send, mate_recv, coef_fsend, coef_frecv,
    rows_send, rows_recv, out_send, out_recv, gram_send, gram_recv, local_sem,
):
    leaf_dev, basis_rank, leaf_pts = basis_ref.shape
    vec_dev = sam_ref.shape[0]
    parents = leaf_dev // 2
    cap0, cap1 = sendf_ref.shape[1], sendc_ref.shape[1]
    nb = farf_ref.shape[1]
    nbc = farc_ref.shape[1]
    nn = near_ref.shape[1]
    half_leaves, half_parents = leaf_dev // 2, parents // 2
    both = 2 * vec_dev
    chunk = leaf_dev // CHUNKS
    devices, vecs = lax.axis_size("leaf"), lax.axis_size("vec")
    groups, columns = vecs // 2, devices // 2
    me, row = lax.axis_index("leaf"), lax.axis_index("vec")
    h, g = lax.rem(row, 2), lax.div(row, 2)
    partner = {"vec": row + 1 - 2 * h}
    first_leaf, first_parent = h * half_leaves, h * half_parents

    def leaf_peer(step):
        return {"leaf": lax.rem(me + step, devices)}

    def group_peer(step):
        return {"vec": lax.rem(g + step, groups) * 2 + h}

    def remote(src, dst, send, recv, peer):
        return pltpu.make_async_remote_copy(
            src_ref=src, dst_ref=dst, send_sem=send, recv_sem=recv,
            device_id=peer, device_id_type=MESH,
        )

    def cut(leaf):
        return pl.ds(pl.multiple_of(leaf * leaf_pts, leaf_pts), leaf_pts)

    def nt(a, b):
        return lax.dot_general(a, b, NT, preferred_element_type=jnp.float32)

    loads = [
        pltpu.make_async_copy(src, dst, local_sem.at[n])
        for n, (src, dst) in enumerate([
            (coords_hbm, coords_ref), (area_hbm, area_ref), (weight_hbm, weight_ref), (sam_hbm, sam_ref),
            (sendf_hbm, sendf_ref), (sendc_hbm, sendc_ref), (basis_hbm, basis_ref), (transfer_hbm, transfer_ref),
            (cf_hbm.at[pl.ds(first_leaf, half_leaves)], cf_ref),
            (cc_hbm.at[pl.ds(first_parent, half_parents)], cc_ref),
            (near_hbm, near_ref), (farf_hbm, farf_ref), (farc_hbm, farc_ref),
        ])
    ]
    for load in loads:
        load.start()
    barrier = pltpu.get_barrier_semaphore()

    def greet(step, carry):
        pl.semaphore_signal(barrier, inc=1, device_id=leaf_peer(step), device_id_type=MESH)
        return carry

    lax.fori_loop(1, devices, greet, 0)
    pl.semaphore_signal(barrier, inc=1, device_id=partner, device_id_type=MESH)
    for step in range(1, groups):
        pl.semaphore_signal(barrier, inc=1, device_id=group_peer(step), device_id_type=MESH)

    for load in loads[:6]:
        load.wait()

    def own(leaf, carry):
        xyz = coords_ref[:, cut(leaf)]
        norm = jnp.sum(xyz * xyz, axis=0, keepdims=True) + area_ref[:, cut(leaf)]
        geo_all[leaf_dev + leaf] = jnp.concatenate([xyz, norm], axis=0)
        weight = weight_ref[:, cut(leaf)] * (1.0 / four_pi)
        scaled = sam_ref[:, cut(leaf)].astype(jnp.float32) * weight
        wvec[leaf_dev + leaf, h] = scaled.astype(jnp.bfloat16)
        return carry

    lax.fori_loop(0, leaf_dev, own, 0, unroll=4)
    table[...] = jnp.zeros_like(table)

    def fill(d, carry):
        table[d, 0:1, 0:cap0] = sendf_ref[pl.ds(d, 1), :]
        table[d, 1:2, 0:cap1] = sendc_ref[pl.ds(d, 1), :]
        return carry

    lax.fori_loop(0, devices, fill, 0)
    got[me] = table[me]
    pl.semaphore_wait(barrier, devices - 1 + 1 + groups - 1)

    odd = lax.rem(me, 2)
    mate = {"leaf": me + 1 - 2 * odd}
    from_mate, from_relay = 2 * (1 - odd), 2 * odd
    onward = {"leaf": me + 2 - 4 * odd}
    sends_on = jnp.where(odd == 0, me + 2 < devices, me >= 2)
    gets_relay = jnp.where(odd == 0, me >= 2, me + 2 < devices)

    def geo_part(part):
        return geo_all.at[pl.ds(part * leaf_dev + first_leaf, half_leaves)]

    def sam_part(part, c):
        return wvec.at[pl.ds(part * leaf_dev + c * chunk, chunk), h]

    def geo_copy():
        return remote(geo_part(1), geo_part(from_relay), geo_send.at[0], geo_recv.at[0], mate)

    def geo_relay():
        return remote(geo_part(from_mate), geo_part(from_relay), geo_send.at[1], geo_recv.at[1], onward)

    def geo_forward(part, n):
        return remote(geo_part(part), geo_part(part), geo_fsend.at[n], geo_frecv.at[n], partner)

    def sam_copy(c):
        return remote(sam_part(1, c), sam_part(from_relay, c), sam_send.at[0, c], sam_recv.at[0, c], mate)

    def sam_relay(c):
        return remote(sam_part(from_mate, c), sam_part(from_relay, c), sam_send.at[1, c], sam_recv.at[1, c], onward)

    def sam_forward(part, n, c):
        block = sam_part(part, c)
        return remote(block, block, sam_fsend.at[n, c], sam_frecv.at[n, c], partner)

    def own_forward():
        block = wvec.at[pl.ds(leaf_dev, leaf_dev), h]
        return remote(block, block, own_send.at[0], own_recv.at[0], partner)

    def table_copy(step):
        peer = lax.rem(me + step, devices)
        return remote(table.at[peer], got.at[me], table_send.at[step], table_recv.at[step], {"leaf": peer})

    def same(step):
        return lax.rem(me + 2 * step, devices)

    def block_from(step):
        return lax.rem(me - 2 * step + devices, devices)

    def mate_block(step):
        return lax.rem(me + 1 - 2 * odd - 2 * step + devices, devices)

    def coef_copy(step):
        part = coef_pk.at[me, :, h]
        return remote(part, part, coef_send.at[step], coef_recv.at[step], {"leaf": same(step)})

    def coef_across(step):
        part = coef_pk.at[block_from(step), :, h]
        return remote(part, part, mate_send.at[step], mate_recv.at[step], mate)

    def coef_forward(step):
        part = coef_pk.at[block_from(step), :, h]
        return remote(part, part, coef_fsend.at[0, step], coef_frecv.at[0, step], partner)

    def mate_forward(step):
        part = coef_pk.at[mate_block(step), :, h]
        return remote(part, part, coef_fsend.at[1, step], coef_frecv.at[1, step], partner)

    geo_copy().start()
    for c in range(CHUNKS):
        sam_copy(c).start()
    own_forward().start()

    def start_table(step, carry):
        table_copy(step).start()
        return carry

    lax.fori_loop(1, devices, start_table, 0)

    loads[6].wait()
    loads[7].wait()
    blank = jnp.zeros((basis_rank, leaf_pts), jnp.bfloat16)
    packed = []
    for m in range(parents):
        left = jnp.concatenate([basis_ref[2 * m], blank], axis=0)
        right = jnp.concatenate([blank, basis_ref[2 * m + 1]], axis=0)
        coef = nt(sam_ref[:, cut(2 * m)], left) + nt(sam_ref[:, cut(2 * m + 1)], right)
        coef = coef.astype(jnp.bfloat16)
        coef_pk[me, m, h] = coef
        packed.append(coef)
    coarse = []
    for m in range(parents):
        both_children = transfer_ref[m].reshape(2 * basis_rank, basis_rank)
        coarse.append(jnp.dot(packed[m], both_children, preferred_element_type=jnp.float32))
    for m in range(half_parents):
        pair = jnp.concatenate([coarse[2 * m], coarse[2 * m + 1]], axis=1)
        coef_pk[me, parents + m, h] = pair.astype(jnp.bfloat16)

    def start_coef(step, carry):
        coef_copy(step).start()
        return carry

    lax.fori_loop(1, columns, start_coef, 0)
    coef_across(0).start()
    coef_forward(0).start()

    def prepare(part):
        def source(leaf, carry):
            geo = geo_all[part * leaf_dev + leaf]
            ones = jnp.ones((1, leaf_pts), jnp.float32)
            rows = jnp.concatenate([geo, ones, jnp.zeros((3, leaf_pts), jnp.float32)], axis=0)
            y1, y2, y3 = pieces(rows)
            rows = jnp.concatenate([y1, y1, y1, y2, y2, y3], axis=0)
            yfeat[part * leaf_dev + leaf] = rows.T.astype(jnp.bfloat16)
            return carry

        lax.fori_loop(0, leaf_dev, source, 0, unroll=4)

    prepare(1)

    def target(leaf, carry):
        xyz = geo_all[leaf_dev + first_leaf + leaf][0:3]
        norm = jnp.sum(xyz * xyz, axis=0, keepdims=True)
        x8 = jnp.concatenate(
            [-2.0 * xyz, jnp.ones_like(norm), norm, jnp.zeros_like(xyz)], axis=0
        )
        x1, x2, x3 = pieces(x8)
        features = jnp.concatenate([x1, x2, x3, x1, x2, x1], axis=0).astype(jnp.bfloat16)
        xfeat[0, leaf] = features
        xfeat[1, leaf] = features
        return carry

    lax.fori_loop(0, half_leaves, target, 0, unroll=2)

    def pass_coef(step, carry):
        coef_copy(step).wait_recv()
        coef_across(step).start()
        coef_forward(step).start()
        return carry

    def pass_mate_sam(c):
        sam_copy(c).wait_recv()

        @pl.when(sends_on)
        def _():
            sam_relay(c).start()

        sam_forward(from_mate, 0, c).start()

    geo_copy().wait_recv()

    @pl.when(sends_on)
    def _():
        geo_relay().start()

    geo_forward(from_mate, 0).start()
    pass_mate_sam(0)
    geo_forward(from_mate, 0).wait_recv()
    prepare(from_mate)
    for c in range(1, CHUNKS):
        pass_mate_sam(c)
    lax.fori_loop(1, columns, pass_coef, 0)

    @pl.when(gets_relay)
    def _():
        geo_relay().wait_recv()
        geo_forward(from_relay, 1).start()
        geo_forward(from_relay, 1).wait_recv()
        prepare(from_relay)
        for c in range(CHUNKS):
            sam_relay(c).wait_recv()
            sam_forward(from_relay, 1, c).start()

    own_forward().wait_recv()
    for c in range(CHUNKS):
        sam_forward(from_mate, 0, c).wait_recv()

    @pl.when(gets_relay)
    def _():
        for c in range(CHUNKS):
            sam_forward(from_relay, 1, c).wait_recv()

    loads[10].wait()

    def near_pair(m):
        base = (me - 1) * leaf_dev
        work = [(s, n) for s in range(2) for n in range(nn)]
        picked = [
            jnp.clip(near_ref[first_leaf + 2 * m + s, n] - base, 0, 3 * leaf_dev - 1) for s, n in work
        ]
        totals, dists = {}, {}
        for step in range(len(work) + LAG):
            if step < len(work):
                s, n = work[step]
                features = xfeat[n % 2, 2 * m + s]
                dists[step] = jnp.dot(yfeat[picked[step]], features, preferred_element_type=jnp.float32)
            if step >= LAG:
                s, n = work[step - LAG]
                block = lax.rsqrt(dists.pop(step - LAG).astype(jnp.bfloat16))
                values = wvec[picked[step - LAG]].reshape(both, leaf_pts)
                term = jnp.dot(values, block, preferred_element_type=jnp.float32)
                totals[s, n % 2] = term if n < 2 else totals[s, n % 2] + term
        for (s, lane), total in totals.items():
            near_all[lane, 2 * m + s] = total

    def pass_mate(step, carry):
        coef_across(step).wait_recv()
        mate_forward(step).start()
        return carry

    def fine_term(leaf, b):
        slot = farf_ref[first_leaf + leaf, b]
        source = lax.div(slot, cap0)
        index = source * leaf_dev + got_smem[source, 0, lax.rem(slot, cap0)]
        return nt(fine_all[index], cf_ref[leaf, b])

    def coarse_term(m, b):
        slot = farc_ref[first_parent + m, b]
        source = lax.div(slot, cap1)
        index = source * parents + got_smem[source, 1, lax.rem(slot, cap1)]
        return nt(coarse_all[index], cc_ref[m, b])

    def rows_copy(m, step):
        part = rows_all.at[g, :, :, pl.ds(pl.multiple_of(m * 2 * leaf_pts, 2 * leaf_pts), 2 * leaf_pts)]
        return remote(part, part, rows_send.at[step, m], rows_recv.at[step, m], group_peer(step))

    def out_copy(m):
        columns = pl.ds(pl.multiple_of(m * 2 * leaf_pts, 2 * leaf_pts), 2 * leaf_pts)
        start = (first_leaf + 2 * m) * leaf_pts
        there = pl.ds(pl.multiple_of(start, 2 * leaf_pts), 2 * leaf_pts)
        return remote(
            rows_all.at[g, 1 - h, :, columns], out_ref.at[:, there], out_send.at[m], out_recv.at[m], partner
        )

    def far_field():
        def finish(step, carry):
            table_copy(step).wait()
            return carry

        def arrive(step, carry):
            coef_forward(step).wait_recv()
            mate_forward(step).wait_recv()
            return carry

        lax.fori_loop(1, devices, finish, 0)
        lax.fori_loop(0, columns, arrive, 0)
        to_smem = pltpu.make_async_copy(got, got_smem, local_sem.at[13])
        to_smem.start()

        def unpack(d, carry):
            for m in range(parents):
                pair = coef_pk[d, m].reshape(both, 2 * basis_rank)
                fine_all[d * leaf_dev + 2 * m] = pair[:, :basis_rank]
                fine_all[d * leaf_dev + 2 * m + 1] = pair[:, basis_rank:]
            for m in range(half_parents):
                pair = coef_pk[d, parents + m].reshape(both, 2 * basis_rank)
                coarse_all[d * parents + 2 * m] = pair[:, :basis_rank]
                coarse_all[d * parents + 2 * m + 1] = pair[:, basis_rank:]
            return carry

        lax.fori_loop(0, devices, unpack, 0)
        for n in (8, 9, 11, 12):
            loads[n].wait()
        to_smem.wait()
        coarse_field = []
        for m in range(half_parents):
            field = coarse_term(m, 0)
            for b in range(1, nbc):
                field = field + coarse_term(m, b)
            coarse_field.append(field.astype(jnp.bfloat16))
        for leaf in range(half_leaves):
            field = nt(coarse_field[leaf // 2], transfer_ref[first_parent + leaf // 2, leaf % 2])
            for b in range(nb):
                field = field + fine_term(leaf, b)
            local_ref[leaf] = field.astype(jnp.bfloat16)

    def emit(m):
        for s in range(2):
            leaf = 2 * m + s
            far = jnp.dot(local_ref[leaf], basis_ref[first_leaf + leaf], preferred_element_type=jnp.float32)
            result = (near_all[0, leaf] + near_all[1, leaf] + far).astype(out_ref.dtype)
            result = result.reshape(2, vec_dev, leaf_pts)
            rows_all[g, :, :, cut(leaf)] = result
        for step in range(1, groups):
            rows_copy(m, step).start()
        out_copy(m).start()

    def near_step(m, carry):
        near_pair(m)

        @pl.when(m == MATE_AT)
        def _():
            lax.fori_loop(0, columns, pass_mate, 0)

        @pl.when(m == FAR_AT)
        def _():
            far_field()
            for done in range(FAR_AT):
                emit(done)

        @pl.when(m >= FAR_AT)
        def _():
            emit(m)
        return carry

    lax.fori_loop(0, half_parents, near_step, 0)

    for leaf in range(half_leaves):
        out_ref[:, cut(first_leaf + leaf)] = rows_all[g, h, :, cut(leaf)]

    def gram_pair(m, carry):
        for step in range(1, groups):
            rows_copy(m, step).wait()
        for s in range(2):
            leaf = 2 * m + s
            everyone = rows_all[:, :, :, cut(leaf)].reshape(vecs * vec_dev, leaf_pts)
            gram_ref[first_leaf + leaf] = nt(rows_all[g, h, :, cut(leaf)], everyone) * (1.0 / leaf_pts)
            gram_out[leaf] = nt(rows_all[g, 1 - h, :, cut(leaf)], everyone) * (1.0 / leaf_pts)
        return carry

    lax.fori_loop(0, half_parents, gram_pair, 0)
    gram_copy = remote(
        gram_out, gram_ref.at[pl.ds(first_leaf, half_leaves)], gram_send.at[0], gram_recv.at[0], partner
    )
    gram_copy.start()

    geo_copy().wait_send()
    geo_forward(from_mate, 0).wait_send()
    own_forward().wait_send()
    for c in range(CHUNKS):
        sam_copy(c).wait_send()
        sam_forward(from_mate, 0, c).wait_send()

    @pl.when(sends_on)
    def _():
        geo_relay().wait_send()
        for c in range(CHUNKS):
            sam_relay(c).wait_send()

    @pl.when(gets_relay)
    def _():
        geo_forward(from_relay, 1).wait_send()
        for c in range(CHUNKS):
            sam_forward(from_relay, 1, c).wait_send()

    def drain(step, carry):
        coef_across(step).wait_send()
        coef_forward(step).wait_send()
        mate_forward(step).wait_send()
        return carry

    def drain_copy(step, carry):
        coef_copy(step).wait_send()
        return carry

    lax.fori_loop(0, columns, drain, 0)
    lax.fori_loop(1, columns, drain_copy, 0)
    for m in range(half_parents):
        out_copy(m).wait()
    gram_copy.wait()


def per_device(
    samples, coords, panel_area, quad_weight, leaf_basis, transfer,
    coupling_fine, coupling_coarse, near_list, send_fine, send_coarse, far_fine, far_coarse,
):
    vec_dev, points = samples.shape
    leaf_dev, basis_rank, leaf_pts = leaf_basis.shape
    parents, half = leaf_dev // 2, leaf_dev // 2
    devices, vecs = lax.axis_size("leaf"), lax.axis_size("vec")
    groups, both = vecs // 2, 2 * vec_dev
    nb, nbc = coupling_fine.shape[1], coupling_coarse.shape[1]
    vmem = pl.BlockSpec(memory_space=pltpu.VMEM)
    hbm = pl.BlockSpec(memory_space=pl.ANY)
    bf16, f32 = jnp.bfloat16, jnp.float32
    dma = pltpu.SemaphoreType.DMA
    sample_out, gram = pl.pallas_call(
        main_kernel,
        out_shape=(
            jax.ShapeDtypeStruct((vec_dev, points), bf16),
            jax.ShapeDtypeStruct((leaf_dev, vec_dev, vecs * vec_dev), f32),
        ),
        in_specs=[hbm] * 13,
        out_specs=(vmem, vmem),
        scratch_shapes=[
            pltpu.SMEM(near_list.shape, jnp.int32),
            pltpu.SMEM(far_fine.shape, jnp.int32),
            pltpu.SMEM(far_coarse.shape, jnp.int32),
            pltpu.VMEM(coords.shape, f32),
            pltpu.VMEM((1, points), f32),
            pltpu.VMEM((1, points), f32),
            pltpu.VMEM(samples.shape, bf16),
            pltpu.VMEM(send_fine.shape, jnp.int32),
            pltpu.VMEM(send_coarse.shape, jnp.int32),
            pltpu.VMEM(transfer.shape, bf16),
            pltpu.VMEM(leaf_basis.shape, bf16),
            pltpu.VMEM((3 * leaf_dev, 4, leaf_pts), f32),
            pltpu.VMEM((3 * leaf_dev, 2, vec_dev, leaf_pts), bf16),
            pltpu.VMEM((devices, 2, 128), jnp.int32),
            pltpu.VMEM((devices, 2, 128), jnp.int32),
            pltpu.SMEM((devices, 2, 128), jnp.int32),
            pltpu.VMEM((devices, parents + parents // 2, 2, vec_dev, 2 * basis_rank), bf16),
            pltpu.VMEM((devices * leaf_dev, both, basis_rank), bf16),
            pltpu.VMEM((devices * parents, both, basis_rank), bf16),
            pltpu.VMEM((half, nb, basis_rank, basis_rank), bf16),
            pltpu.VMEM((half // 2, nbc, basis_rank, basis_rank), bf16),
            pltpu.VMEM((3 * leaf_dev, leaf_pts, 48), bf16),
            pltpu.VMEM((2, half, 48, leaf_pts), bf16),
            pltpu.VMEM((2, half, both, leaf_pts), f32),
            pltpu.VMEM((half, both, basis_rank), bf16),
            pltpu.VMEM((groups, 2, vec_dev, half * leaf_pts), bf16),
            pltpu.VMEM((half, vec_dev, vecs * vec_dev), f32),
            dma((2,)), dma((2,)), dma((2,)), dma((2,)),
            dma((2, CHUNKS)), dma((2, CHUNKS)), dma((2, CHUNKS)), dma((2, CHUNKS)), dma((1,)), dma((1,)),
            dma((devices,)), dma((devices,)),
            dma((devices // 2,)), dma((devices // 2,)), dma((devices // 2,)), dma((devices // 2,)),
            dma((2, devices // 2)), dma((2, devices // 2)),
            dma((groups, half // 2)), dma((groups, half // 2)),
            dma((half // 2,)), dma((half // 2,)),
            dma((1,)), dma((1,)),
            dma((14,)),
        ],
        compiler_params=pltpu.CompilerParams(
            vmem_limit_bytes=56 * 1024 * 1024, collective_id=0, has_side_effects=True
        ),
    )(
        near_list, far_fine, far_coarse,
        coords, panel_area[None, :], quad_weight[None, :], samples, send_fine, send_coarse,
        transfer, leaf_basis, coupling_fine, coupling_coarse,
    )
    return sample_out, gram


def solution(mesh):
    return jax.shard_map(
        per_device,
        mesh=mesh,
        in_specs=(
            P("vec", "leaf"), P(None, "leaf"), P("leaf"), P("leaf"),
            P("leaf", None, None), P("leaf", None, None, None),
            P("leaf", None, None, None), P("leaf", None, None, None),
            P("leaf", None), P("leaf", None), P("leaf", None), P("leaf", None), P("leaf", None),
        ),
        out_specs=(P("vec", "leaf"), P("leaf", "vec", None)),
        check_vma=False,
    )
```

time: 39.8 us -> 34.8 us (0.87)
  the two profiles are of different devices: /device:TPU:11 before, /device:TPU:3 now
where the time goes in v2:
time: 34.8 us; the launch traced here: 34.4 us
  Pallas kernels  30.7 us (88%)
  local copies, waits for them, and re-layouts  3.14 us (9%)
  between operations  0.64 us (2%)
    pallas_call x1, Pallas kernels, per_device(): pl.pallas_call(main_kernel, out_shape=(jax.ShapeDtypeStruct((vec_dev, poi...  30.7 us
    unnamed x2, local copies, waits for them, and re-layouts  3.14 us

profile of v2, /device:TPU:3, one launch (start us, length us, event | category | flops | bytes accessed | tf_op | source)
XLA Modules:
  0.0 34.4 jit_solution(17624873639244558800)
XLA Ops:
  0.6 30.7 %shard_map.140 = (bf16[16,4096]{1,0:T(8,128)(2,1)}, f32[16,16,64]{2,1,0:T(8,128)}) custom-call(s32[16,16]{1,0:T(8,128)} %near_hbm.1, s32[16,16]{1,0:T(8,128)} %farf_hbm.1, s32[8,16]{1,0:T(8,128)} %farc_hbm.1, f32[3,4096]{1,0:T(4,128)} %coords_hbm.1, f32[1,4096]{1,0:T(1,128)} %bitcast.2, f32[1,4096]{1,0:T(1,128)} %bitcast.3, bf16[16,4096]{1,0:T(8,128)(2,1)} %sam_hbm.1, ...), custom_call_target="tpu_custom_call" | custom-call | tf_op jit(solution)/shard_map/pallas_call | solution.py:491
  31.3 1.6 %copy.17 = bf16[16,4096]{1,0:T(8,128)(2,1)} copy(bf16[16,4096]{1,0:T(8,128)(2,1)} %get-tuple-element.4) | data formatting | bytes 262144
  32.9 1.6 %copy.18 = f32[16,16,64]{2,1,0:T(8,128)} copy(f32[16,16,64]{2,1,0:T(8,128)} %get-tuple-element.5) | data formatting | bytes 131072

commit v3 on v2

--- a/solution.py
+++ b/solution.py
@@ -11,6 +11,9 @@
 MESH = pl.DeviceIdType.MESH
 LAG = 4
 CHUNKS = 4
+DIRECT = 1
+GEO_DIRECT = False
+RELAYED = CHUNKS - DIRECT
 MATE_AT, FAR_AT = 1, 2
 
 
@@ -119,6 +122,7 @@
     mate = {"leaf": me + 1 - 2 * odd}
     from_mate, from_relay = 2 * (1 - odd), 2 * odd
     onward = {"leaf": me + 2 - 4 * odd}
+    other = {"leaf": me - 1 + 2 * odd}
     sends_on = jnp.where(odd == 0, me + 2 < devices, me >= 2)
     gets_relay = jnp.where(odd == 0, me >= 2, me + 2 < devices)
 
@@ -132,6 +136,8 @@
         return remote(geo_part(1), geo_part(from_relay), geo_send.at[0], geo_recv.at[0], mate)
 
     def geo_relay():
+        if GEO_DIRECT:
+            return remote(geo_part(1), geo_part(from_mate), geo_send.at[1], geo_recv.at[1], other)
         return remote(geo_part(from_mate), geo_part(from_relay), geo_send.at[1], geo_recv.at[1], onward)
 
     def geo_forward(part, n):
@@ -142,6 +148,9 @@
 
     def sam_relay(c):
         return remote(sam_part(from_mate, c), sam_part(from_relay, c), sam_send.at[1, c], sam_recv.at[1, c], onward)
+
+    def sam_direct(c):
+        return remote(sam_part(1, c), sam_part(from_mate, c), sam_send.at[1, c], sam_recv.at[1, c], other)
 
     def sam_forward(part, n, c):
         block = sam_part(part, c)
@@ -181,7 +190,20 @@
         return remote(part, part, coef_fsend.at[1, step], coef_frecv.at[1, step], partner)
 
     geo_copy().start()
-    for c in range(CHUNKS):
+    if GEO_DIRECT:
+
+        @pl.when(gets_relay)
+        def _():
+            geo_relay().start()
+
+    sam_copy(0).start()
+
+    @pl.when(gets_relay)
+    def _():
+        for c in range(RELAYED, CHUNKS):
+            sam_direct(c).start()
+
+    for c in range(1, CHUNKS):
         sam_copy(c).start()
     own_forward().start()
 
@@ -255,17 +277,21 @@
     def pass_mate_sam(c):
         sam_copy(c).wait_recv()
 
+        if c < RELAYED:
+
+            @pl.when(sends_on)
+            def _():
+                sam_relay(c).start()
+
+        sam_forward(from_mate, 0, c).start()
+
+    geo_copy().wait_recv()
+
+    if not GEO_DIRECT:
+
         @pl.when(sends_on)
         def _():
-            sam_relay(c).start()
-
-        sam_forward(from_mate, 0, c).start()
-
-    geo_copy().wait_recv()
-
-    @pl.when(sends_on)
-    def _():
-        geo_relay().start()
+            geo_relay().start()
 
     geo_forward(from_mate, 0).start()
     pass_mate_sam(0)
@@ -372,7 +398,7 @@
                 coarse_all[d * parents + 2 * m + 1] = pair[:, basis_rank:]
             return carry
 
-        lax.fori_loop(0, devices, unpack, 0)
+        lax.fori_loop(0, devices, unpack, 0, unroll=4)
         for n in (8, 9, 11, 12):
             loads[n].wait()
         to_smem.wait()
@@ -383,9 +409,10 @@
                 field = field + coarse_term(m, b)
             coarse_field.append(field.astype(jnp.bfloat16))
         for leaf in range(half_leaves):
-            field = nt(coarse_field[leaf // 2], transfer_ref[first_parent + leaf // 2, leaf % 2])
-            for b in range(nb):
+            field = fine_term(leaf, 0)
+            for b in range(1, nb):
                 field = field + fine_term(leaf, b)
+            field = field + nt(coarse_field[leaf // 2], transfer_ref[first_parent + leaf // 2, leaf % 2])
             local_ref[leaf] = field.astype(jnp.bfloat16)
 
     def emit(m):
@@ -445,14 +472,19 @@
         sam_copy(c).wait_send()
         sam_forward(from_mate, 0, c).wait_send()
 
+    @pl.when(gets_relay if GEO_DIRECT else sends_on)
+    def _():
+        geo_relay().wait_send()
+
     @pl.when(sends_on)
     def _():
-        geo_relay().wait_send()
-        for c in range(CHUNKS):
+        for c in range(RELAYED):
             sam_relay(c).wait_send()
 
     @pl.when(gets_relay)
     def _():
+        for c in range(RELAYED, CHUNKS):
+            sam_direct(c).wait_send()
         geo_forward(from_relay, 1).wait_send()
         for c in range(CHUNKS):
             sam_forward(from_relay, 1, c).wait_send()
@@ -472,6 +504,17 @@
     for m in range(half_parents):
         out_copy(m).wait()
     gram_copy.wait()
+
+
+def write_kernel(out_ref, gram_ref, out_hbm, gram_hbm, sem):
+    copies = [
+        pltpu.make_async_copy(out_ref, out_hbm, sem.at[0]),
+        pltpu.make_async_copy(gram_ref, gram_hbm, sem.at[1]),
+    ]
+    for copy in copies:
+        copy.start()
+    for copy in copies:
+        copy.wait()
 
 
 def per_device(
@@ -491,8 +534,8 @@
     sample_out, gram = pl.pallas_call(
         main_kernel,
         out_shape=(
-            jax.ShapeDtypeStruct((vec_dev, points), bf16),
-            jax.ShapeDtypeStruct((leaf_dev, vec_dev, vecs * vec_dev), f32),
+            pltpu.VMEM((vec_dev, points), bf16),
+            pltpu.VMEM((leaf_dev, vec_dev, vecs * vec_dev), f32),
         ),
         in_specs=[hbm] * 13,
         out_specs=(vmem, vmem),
@@ -542,7 +585,16 @@
         coords, panel_area[None, :], quad_weight[None, :], samples, send_fine, send_coarse,
         transfer, leaf_basis, coupling_fine, coupling_coarse,
     )
-    return sample_out, gram
+    return pl.pallas_call(
+        write_kernel,
+        out_shape=(
+            jax.ShapeDtypeStruct(sample_out.shape, bf16),
+            jax.ShapeDtypeStruct(gram.shape, f32),
+        ),
+        in_specs=[vmem] * 2,
+        out_specs=(hbm, hbm),
+        scratch_shapes=[dma((2,))],
+    )(pltpu.with_memory_space_constraint(sample_out, pltpu.VMEM), pltpu.with_memory_space_constraint(gram, pltpu.VMEM))
 
 
 def solution(mesh):

time: 34.8 us -> 31.3 us (0.90)
  local copies, waits for them, and re-layouts: 3.14 us -> 0 us
  Pallas kernels: 30.7 us -> 30.2 us
    unnamed x2 -> x0, local copies, waits for them, and re-layouts: 3.14 us -> none
    pallas_call x1 -> x2, Pallas kernels: 30.7 us -> 30.2 us  [the longest x1 29.4 us: per_device(): pl.pallas_call(main_kernel, out_shape=(pltpu.VMEM((vec_dev, points), bf16...]
where the time goes in v3:
time: 31.3 us; the launch traced here: 30.8 us
  Pallas kernels  30.2 us (96%)
  between operations  0.64 us (2%)
    pallas_call x1, Pallas kernels, per_device(): pl.pallas_call(main_kernel, out_shape=(pltpu.VMEM((vec_dev, points), bf16...  29.4 us
    pallas_call x1, Pallas kernels, per_device(): pl.pallas_call(write_kernel, out_shape=(jax.ShapeDtypeStruct(sample_out.s...  0.72 us

profile of v3, /device:TPU:3, one launch (start us, length us, event | category | flops | bytes accessed | tf_op | source)
XLA Modules:
  0.0 30.8 jit_solution(8923490427946598298)
XLA Ops:
  0.6 29.4 %shard_map.140 = (bf16[16,4096]{1,0:T(8,128)(2,1)S(1)}, f32[16,16,64]{2,1,0:T(8,128)S(1)}) custom-call(s32[16,16]{1,0:T(8,128)} %near_hbm.1, s32[16,16]{1,0:T(8,128)} %farf_hbm.1, s32[8,16]{1,0:T(8,128)} %farc_hbm.1, f32[3,4096]{1,0:T(4,128)} %coords_hbm.1, f32[1,4096]{1,0:T(1,128)} %bitcast.2, f32[1,4096]{1,0:T(1,128)} %bitcast.3, ...), custom_call_target="tpu_custom_call" | custom-call | tf_op jit(solution)/shard_map/pallas_call | solution.py:534
  30.1 0.7 %shard_map.141 = (bf16[16,4096]{1,0:T(8,128)(2,1)}, f32[16,16,64]{2,1,0:T(8,128)}) custom-call(bf16[16,4096]{1,0:T(8,128)(2,1)S(1)} %get-tuple-element.4.out_ref, f32[16,16,64]{2,1,0:T(8,128)S(1)} %get-tuple-element.5.gram_ref), custom_call_target="tpu_custom_call" | custom-call | tf_op jit(solution)/shard_map/pallas_call | solution.py:588

commit v4 on v3

--- a/solution.py
+++ b/solution.py
@@ -9,7 +9,7 @@
 four_pi = 4.0 * 3.141592653589793
 NT = (((1,), (1,)), ((), ()))
 MESH = pl.DeviceIdType.MESH
-LAG = 4
+LAG = 6
 CHUNKS = 4
 DIRECT = 1
 GEO_DIRECT = False
@@ -30,7 +30,7 @@
     out_ref, gram_ref,
     near_ref, farf_ref, farc_ref,
     coords_ref, area_ref, weight_ref, sam_ref, sendf_ref, sendc_ref, transfer_ref, basis_ref,
-    geo_all, wvec, table, got, got_smem, coef_pk, fine_all, coarse_all, cf_ref, cc_ref,
+    geo_all, wvec, table, got, got_smem, coef_pk, fine_tab, coarse_tab, cf_ref, cc_ref, cf_pair, cc_pair,
     yfeat, xfeat, near_all, local_ref, rows_all, gram_out,
     geo_send, geo_recv, geo_fsend, geo_frecv, sam_send, sam_recv, sam_fsend, sam_frecv, own_send, own_recv,
     table_send, table_recv, coef_send, coef_recv, mate_send, mate_recv, coef_fsend, coef_frecv,
@@ -144,17 +144,23 @@
         return remote(geo_part(part), geo_part(part), geo_fsend.at[n], geo_frecv.at[n], partner)
 
     def sam_copy(c):
-        return remote(sam_part(1, c), sam_part(from_relay, c), sam_send.at[0, c], sam_recv.at[0, c], mate)
+        return remote(sam_part(1, c), sam_part(from_relay, c), sam_send.at[0], sam_recv.at[0, c], mate)
 
     def sam_relay(c):
-        return remote(sam_part(from_mate, c), sam_part(from_relay, c), sam_send.at[1, c], sam_recv.at[1, c], onward)
+        return remote(sam_part(from_mate, c), sam_part(from_relay, c), sam_send.at[1], sam_recv.at[1, c], onward)
 
     def sam_direct(c):
-        return remote(sam_part(1, c), sam_part(from_mate, c), sam_send.at[1, c], sam_recv.at[1, c], other)
+        return remote(sam_part(1, c), sam_part(from_mate, c), sam_send.at[2], sam_recv.at[1, c], other)
 
     def sam_forward(part, n, c):
         block = sam_part(part, c)
-        return remote(block, block, sam_fsend.at[n, c], sam_frecv.at[n, c], partner)
+        return remote(block, block, sam_fsend.at[n], sam_frecv.at[n], partner)
+
+    def settle(ref, send, recv):
+        return remote(ref, ref, send, recv, partner)
+
+    def chunks(part, count):
+        return wvec.at[pl.ds(part * leaf_dev, count * chunk), h]
 
     def own_forward():
         block = wvec.at[pl.ds(leaf_dev, leaf_dev), h]
@@ -162,7 +168,7 @@
 
     def table_copy(step):
         peer = lax.rem(me + step, devices)
-        return remote(table.at[peer], got.at[me], table_send.at[step], table_recv.at[step], {"leaf": peer})
+        return remote(table.at[peer], got.at[me], table_send.at[0], table_recv.at[0], {"leaf": peer})
 
     def same(step):
         return lax.rem(me + 2 * step, devices)
@@ -175,19 +181,19 @@
 
     def coef_copy(step):
         part = coef_pk.at[me, :, h]
-        return remote(part, part, coef_send.at[step], coef_recv.at[step], {"leaf": same(step)})
+        return remote(part, part, coef_send.at[0], coef_recv.at[step], {"leaf": same(step)})
 
     def coef_across(step):
         part = coef_pk.at[block_from(step), :, h]
-        return remote(part, part, mate_send.at[step], mate_recv.at[step], mate)
+        return remote(part, part, mate_send.at[0], mate_recv.at[step], mate)
 
     def coef_forward(step):
         part = coef_pk.at[block_from(step), :, h]
-        return remote(part, part, coef_fsend.at[0, step], coef_frecv.at[0, step], partner)
+        return remote(part, part, coef_fsend.at[0], coef_frecv.at[0], partner)
 
     def mate_forward(step):
         part = coef_pk.at[mate_block(step), :, h]
-        return remote(part, part, coef_fsend.at[1, step], coef_frecv.at[1, step], partner)
+        return remote(part, part, coef_fsend.at[0], coef_frecv.at[0], partner)
 
     geo_copy().start()
     if GEO_DIRECT:
@@ -301,10 +307,27 @@
         pass_mate_sam(c)
     lax.fori_loop(1, columns, pass_coef, 0)
 
+    loads[8].wait()
+    loads[9].wait()
+
+    def pair_up(src, dst):
+        def one(i, carry):
+            for b in range(src.shape[1] // 2):
+                dst[i, b] = jnp.concatenate([src[i, 2 * b], src[i, 2 * b + 1]], axis=1)
+            return carry
+
+        lax.fori_loop(0, src.shape[0], one, 0, unroll=2)
+
     @pl.when(gets_relay)
     def _():
         geo_relay().wait_recv()
         geo_forward(from_relay, 1).start()
+
+    pair_up(cf_ref, cf_pair)
+    pair_up(cc_ref, cc_pair)
+
+    @pl.when(gets_relay)
+    def _():
         geo_forward(from_relay, 1).wait_recv()
         prepare(from_relay)
         for c in range(CHUNKS):
@@ -312,13 +335,11 @@
             sam_forward(from_relay, 1, c).start()
 
     own_forward().wait_recv()
-    for c in range(CHUNKS):
-        sam_forward(from_mate, 0, c).wait_recv()
+    settle(chunks(from_mate, CHUNKS), sam_fsend.at[0], sam_frecv.at[0]).wait_recv()
 
     @pl.when(gets_relay)
     def _():
-        for c in range(CHUNKS):
-            sam_forward(from_relay, 1, c).wait_recv()
+        settle(chunks(from_relay, CHUNKS), sam_fsend.at[1], sam_frecv.at[1]).wait_recv()
 
     loads[10].wait()
 
@@ -348,69 +369,69 @@
         mate_forward(step).start()
         return carry
 
+    left_lanes = lax.broadcasted_iota(jnp.int32, (both, 2 * basis_rank), 1) < basis_rank
+
+    def split(slot, cap):
+        if cap & (cap - 1):
+            return lax.div(slot, cap), lax.rem(slot, cap)
+        return slot >> (cap.bit_length() - 1), slot & (cap - 1)
+
+    def pair_term(tab, tiles, far_ref, at, cap, line, per_device, b):
+        rows = []
+        for lane in range(2):
+            slot = far_ref[at, 2 * b + lane]
+            source, place = split(slot, cap)
+            index = source * per_device + got_smem[source, line, place]
+            rows.append(tab[index ^ lane])
+        return nt(jnp.where(left_lanes, rows[0], rows[1]), tiles[b])
+
     def fine_term(leaf, b):
-        slot = farf_ref[first_leaf + leaf, b]
-        source = lax.div(slot, cap0)
-        index = source * leaf_dev + got_smem[source, 0, lax.rem(slot, cap0)]
-        return nt(fine_all[index], cf_ref[leaf, b])
+        return pair_term(fine_tab, cf_pair.at[leaf], farf_ref, first_leaf + leaf, cap0, 0, leaf_dev, b)
 
     def coarse_term(m, b):
-        slot = farc_ref[first_parent + m, b]
-        source = lax.div(slot, cap1)
-        index = source * parents + got_smem[source, 1, lax.rem(slot, cap1)]
-        return nt(coarse_all[index], cc_ref[m, b])
+        return pair_term(coarse_tab, cc_pair.at[m], farc_ref, first_parent + m, cap1, 1, parents, b)
 
     def rows_copy(m, step):
         part = rows_all.at[g, :, :, pl.ds(pl.multiple_of(m * 2 * leaf_pts, 2 * leaf_pts), 2 * leaf_pts)]
-        return remote(part, part, rows_send.at[step, m], rows_recv.at[step, m], group_peer(step))
+        return remote(part, part, rows_send.at[step - 1], rows_recv.at[step - 1, m], group_peer(step))
 
     def out_copy(m):
         columns = pl.ds(pl.multiple_of(m * 2 * leaf_pts, 2 * leaf_pts), 2 * leaf_pts)
         start = (first_leaf + 2 * m) * leaf_pts
         there = pl.ds(pl.multiple_of(start, 2 * leaf_pts), 2 * leaf_pts)
         return remote(
-            rows_all.at[g, 1 - h, :, columns], out_ref.at[:, there], out_send.at[m], out_recv.at[m], partner
+            rows_all.at[g, 1 - h, :, columns], out_ref.at[:, there], out_send.at[0], out_recv.at[0], partner
         )
 
     def far_field():
-        def finish(step, carry):
-            table_copy(step).wait()
-            return carry
-
-        def arrive(step, carry):
-            coef_forward(step).wait_recv()
-            mate_forward(step).wait_recv()
-            return carry
-
-        lax.fori_loop(1, devices, finish, 0)
-        lax.fori_loop(0, columns, arrive, 0)
+        settle(got.at[pl.ds(0, devices - 1)], table_send.at[0], table_recv.at[0]).wait()
+        settle(coef_pk.at[:, :, 1 - h], coef_fsend.at[0], coef_frecv.at[0]).wait_recv()
         to_smem = pltpu.make_async_copy(got, got_smem, local_sem.at[13])
         to_smem.start()
 
         def unpack(d, carry):
-            for m in range(parents):
-                pair = coef_pk[d, m].reshape(both, 2 * basis_rank)
-                fine_all[d * leaf_dev + 2 * m] = pair[:, :basis_rank]
-                fine_all[d * leaf_dev + 2 * m + 1] = pair[:, basis_rank:]
-            for m in range(half_parents):
-                pair = coef_pk[d, parents + m].reshape(both, 2 * basis_rank)
-                coarse_all[d * parents + 2 * m] = pair[:, :basis_rank]
-                coarse_all[d * parents + 2 * m + 1] = pair[:, basis_rank:]
+            for tab, count, first in ((fine_tab, parents, 0), (coarse_tab, half_parents, parents)):
+                for m in range(count):
+                    pair = coef_pk[d, first + m].reshape(both, 2 * basis_rank)
+                    tab[2 * (d * count + m)] = pair
+                    tab[2 * (d * count + m) + 1] = jnp.concatenate(
+                        [pair[:, basis_rank:], pair[:, :basis_rank]], axis=1
+                    )
             return carry
 
         lax.fori_loop(0, devices, unpack, 0, unroll=4)
-        for n in (8, 9, 11, 12):
-            loads[n].wait()
+        loads[11].wait()
+        loads[12].wait()
         to_smem.wait()
         coarse_field = []
         for m in range(half_parents):
             field = coarse_term(m, 0)
-            for b in range(1, nbc):
+            for b in range(1, nbc // 2):
                 field = field + coarse_term(m, b)
             coarse_field.append(field.astype(jnp.bfloat16))
         for leaf in range(half_leaves):
             field = fine_term(leaf, 0)
-            for b in range(1, nb):
+            for b in range(1, nb // 2):
                 field = field + fine_term(leaf, b)
             field = field + nt(coarse_field[leaf // 2], transfer_ref[first_parent + leaf // 2, leaf % 2])
             local_ref[leaf] = field.astype(jnp.bfloat16)
@@ -451,7 +472,7 @@
 
     def gram_pair(m, carry):
         for step in range(1, groups):
-            rows_copy(m, step).wait()
+            rows_copy(m, step).wait_recv()
         for s in range(2):
             leaf = 2 * m + s
             everyone = rows_all[:, :, :, cut(leaf)].reshape(vecs * vec_dev, leaf_pts)
@@ -468,9 +489,8 @@
     geo_copy().wait_send()
     geo_forward(from_mate, 0).wait_send()
     own_forward().wait_send()
-    for c in range(CHUNKS):
-        sam_copy(c).wait_send()
-        sam_forward(from_mate, 0, c).wait_send()
+    settle(chunks(1, CHUNKS), sam_send.at[0], sam_frecv.at[0]).wait_send()
+    settle(chunks(1, CHUNKS), sam_fsend.at[0], sam_frecv.at[0]).wait_send()
 
     @pl.when(gets_relay if GEO_DIRECT else sends_on)
     def _():
@@ -478,31 +498,22 @@
 
     @pl.when(sends_on)
     def _():
-        for c in range(RELAYED):
-            sam_relay(c).wait_send()
+        settle(chunks(1, RELAYED), sam_send.at[1], sam_frecv.at[0]).wait_send()
 
     @pl.when(gets_relay)
     def _():
-        for c in range(RELAYED, CHUNKS):
-            sam_direct(c).wait_send()
+        settle(chunks(1, DIRECT), sam_send.at[2], sam_frecv.at[0]).wait_send()
         geo_forward(from_relay, 1).wait_send()
-        for c in range(CHUNKS):
-            sam_forward(from_relay, 1, c).wait_send()
-
-    def drain(step, carry):
-        coef_across(step).wait_send()
-        coef_forward(step).wait_send()
-        mate_forward(step).wait_send()
-        return carry
-
-    def drain_copy(step, carry):
-        coef_copy(step).wait_send()
-        return carry
-
-    lax.fori_loop(0, columns, drain, 0)
-    lax.fori_loop(1, columns, drain_copy, 0)
-    for m in range(half_parents):
-        out_copy(m).wait()
+        settle(chunks(1, CHUNKS), sam_fsend.at[1], sam_frecv.at[0]).wait_send()
+
+    settle(coef_pk.at[pl.ds(0, columns), :, h], mate_send.at[0], coef_frecv.at[0]).wait_send()
+    settle(coef_pk.at[:, :, h], coef_fsend.at[0], coef_frecv.at[0]).wait_send()
+    settle(coef_pk.at[pl.ds(0, columns - 1), :, h], coef_send.at[0], coef_frecv.at[0]).wait_send()
+    for step in range(1, groups):
+        settle(rows_all.at[g], rows_send.at[step - 1], coef_frecv.at[0]).wait_send()
+    settle(rows_all.at[g, 1 - h], out_send.at[0], out_recv.at[0]).wait_send()
+    theirs = pl.ds(pl.multiple_of((1 - h) * half_leaves * leaf_pts, half_leaves * leaf_pts), half_leaves * leaf_pts)
+    settle(out_ref.at[:, theirs], out_send.at[0], out_recv.at[0]).wait_recv()
     gram_copy.wait()
 
 
@@ -557,10 +568,12 @@
             pltpu.VMEM((devices, 2, 128), jnp.int32),
             pltpu.SMEM((devices, 2, 128), jnp.int32),
             pltpu.VMEM((devices, parents + parents // 2, 2, vec_dev, 2 * basis_rank), bf16),
-            pltpu.VMEM((devices * leaf_dev, both, basis_rank), bf16),
-            pltpu.VMEM((devices * parents, both, basis_rank), bf16),
+            pltpu.VMEM((devices * leaf_dev, both, 2 * basis_rank), bf16),
+            pltpu.VMEM((devices * parents, both, 2 * basis_rank), bf16),
             pltpu.VMEM((half, nb, basis_rank, basis_rank), bf16),
             pltpu.VMEM((half // 2, nbc, basis_rank, basis_rank), bf16),
+            pltpu.VMEM((half, nb // 2, basis_rank, 2 * basis_rank), bf16),
+            pltpu.VMEM((half // 2, nbc // 2, basis_rank, 2 * basis_rank), bf16),
             pltpu.VMEM((3 * leaf_dev, leaf_pts, 48), bf16),
             pltpu.VMEM((2, half, 48, leaf_pts), bf16),
             pltpu.VMEM((2, half, both, leaf_pts), f32),
@@ -568,12 +581,12 @@
             pltpu.VMEM((groups, 2, vec_dev, half * leaf_pts), bf16),
             pltpu.VMEM((half, vec_dev, vecs * vec_dev), f32),
             dma((2,)), dma((2,)), dma((2,)), dma((2,)),
-            dma((2, CHUNKS)), dma((2, CHUNKS)), dma((2, CHUNKS)), dma((2, CHUNKS)), dma((1,)), dma((1,)),
-            dma((devices,)), dma((devices,)),
-            dma((devices // 2,)), dma((devices // 2,)), dma((devices // 2,)), dma((devices // 2,)),
-            dma((2, devices // 2)), dma((2, devices // 2)),
-            dma((groups, half // 2)), dma((groups, half // 2)),
-            dma((half // 2,)), dma((half // 2,)),
+            dma((3,)), dma((2, CHUNKS)), dma((2,)), dma((2,)), dma((1,)), dma((1,)),
+            dma((1,)), dma((1,)),
+            dma((1,)), dma((devices // 2,)), dma((1,)), dma((devices // 2,)),
+            dma((1,)), dma((1,)),
+            dma((groups - 1,)), dma((groups - 1, half // 2)),
+            dma((1,)), dma((1,)),
             dma((1,)), dma((1,)),
             dma((14,)),
         ],

time: 31.3 us -> 29.5 us (0.942)
  Pallas kernels: 30.2 us -> 28.4 us
    pallas_call x1, Pallas kernels: 29.4 us -> 27.7 us  [per_device(): pl.pallas_call(main_kernel, out_shape=(pltpu.VMEM((vec_dev, points), bf16...]
where the time goes in v4:
time: 29.5 us; the launch traced here: 29.1 us
  Pallas kernels  28.4 us (96%)
  between operations  0.64 us (2%)
    pallas_call x1, Pallas kernels, per_device(): pl.pallas_call(main_kernel, out_shape=(pltpu.VMEM((vec_dev, points), bf16...  27.7 us
    pallas_call x1, Pallas kernels, per_device(): pl.pallas_call(write_kernel, out_shape=(jax.ShapeDtypeStruct(sample_out.s...  0.72 us

profile of v4, /device:TPU:3, one launch (start us, length us, event | category | flops | bytes accessed | tf_op | source)
XLA Modules:
  0.0 29.1 jit_solution(17385427023917499957)
XLA Ops:
  0.6 27.7 %shard_map.140 = (bf16[16,4096]{1,0:T(8,128)(2,1)S(1)}, f32[16,16,64]{2,1,0:T(8,128)S(1)}) custom-call(s32[16,16]{1,0:T(8,128)} %near_hbm.1, s32[16,16]{1,0:T(8,128)} %farf_hbm.1, s32[8,16]{1,0:T(8,128)} %farc_hbm.1, f32[3,4096]{1,0:T(4,128)} %coords_hbm.1, f32[1,4096]{1,0:T(1,128)} %bitcast.2, f32[1,4096]{1,0:T(1,128)} %bitcast.3, ...), custom_call_target="tpu_custom_call" | custom-call | tf_op jit(solution)/shard_map/pallas_call | solution.py:545
  28.4 0.7 %shard_map.141 = (bf16[16,4096]{1,0:T(8,128)(2,1)}, f32[16,16,64]{2,1,0:T(8,128)}) custom-call(bf16[16,4096]{1,0:T(8,128)(2,1)S(1)} %get-tuple-element.4.out_ref, f32[16,16,64]{2,1,0:T(8,128)S(1)} %get-tuple-element.5.gram_ref), custom_call_target="tpu_custom_call" | custom-call | tf_op jit(solution)/shard_map/pallas_call | solution.py:601

commit v5 on v4

--- a/solution.py
+++ b/solution.py
@@ -10,8 +10,8 @@
 NT = (((1,), (1,)), ((), ()))
 MESH = pl.DeviceIdType.MESH
 LAG = 6
-CHUNKS = 4
-DIRECT = 1
+CHUNKS = 8
+DIRECT = 2
 GEO_DIRECT = False
 RELAYED = CHUNKS - DIRECT
 MATE_AT, FAR_AT = 1, 2

time: 29.5 us -> 29.3 us (level); the launches traced: 29.1 us -> 29.2 us
  no operation moved by 1% of the time
where the time goes in v5:
time: 29.3 us; the launch traced here: 29.2 us
  Pallas kernels  28.6 us (98%)
  between operations  0.64 us (2%)
    pallas_call x1, Pallas kernels, per_device(): pl.pallas_call(main_kernel, out_shape=(pltpu.VMEM((vec_dev, points), bf16...  27.8 us
    pallas_call x1, Pallas kernels, per_device(): pl.pallas_call(write_kernel, out_shape=(jax.ShapeDtypeStruct(sample_out.s...  0.72 us

profile of v5, /device:TPU:3, one launch (start us, length us, event | category | flops | bytes accessed | tf_op | source)
XLA Modules:
  0.0 29.2 jit_solution(930500780398045841)
XLA Ops:
  0.6 27.8 %shard_map.140 = (bf16[16,4096]{1,0:T(8,128)(2,1)S(1)}, f32[16,16,64]{2,1,0:T(8,128)S(1)}) custom-call(s32[16,16]{1,0:T(8,128)} %near_hbm.1, s32[16,16]{1,0:T(8,128)} %farf_hbm.1, s32[8,16]{1,0:T(8,128)} %farc_hbm.1, f32[3,4096]{1,0:T(4,128)} %coords_hbm.1, f32[1,4096]{1,0:T(1,128)} %bitcast.2, f32[1,4096]{1,0:T(1,128)} %bitcast.3, ...), custom_call_target="tpu_custom_call" | custom-call | tf_op jit(solution)/shard_map/pallas_call | solution.py:545
  28.5 0.7 %shard_map.141 = (bf16[16,4096]{1,0:T(8,128)(2,1)}, f32[16,16,64]{2,1,0:T(8,128)}) custom-call(bf16[16,4096]{1,0:T(8,128)(2,1)S(1)} %get-tuple-element.4.out_ref, f32[16,16,64]{2,1,0:T(8,128)S(1)} %get-tuple-element.5.gram_ref), custom_call_target="tpu_custom_call" | custom-call | tf_op jit(solution)/shard_map/pallas_call | solution.py:601
